TPU v7x, 32 devices: a whole 2x2x4 slice. The times are simulated.
32 devices in a mesh: dof: 8 (over y, x, core), tm: 4 (over z).
Axes of the slice: x: 2, y: 2, z: 4, core: 2. Of those that a mesh axis runs over, the one named last changes fastest.
Arguments:
- snapshots: bfloat16 [163840, 1024], P('dof', 'tm'), may hold values from -6 to 6
- basis: bfloat16 [163840, 64], P('dof'), may hold values from -0.015625 to 0.015625
Outputs:
- gram: float32 [2144, 2144], P('tm', 'dof')
- coords: float32 [64, 1024], P(None, 'tm')
All inputs are finite; a program needn't handle non-finite values.
Results may differ from a plain program's by a relative error of at most 0.0021.
Values may be sent and summed in bfloat16 or wider, within the bound.
No kernel may reach another device: no remote copies, remote signals or barrier semaphores. Data moves between devices by JAX's collectives and lax.ppermute only.
A program may use at most 64 MiB of HBM per device.

v0:
```python
import jax
import jax.numpy as jnp
import numpy as np
from jax import lax
from jax.sharding import PartitionSpec as P


def build_features(coords):
    modes = coords.shape[0]
    upper_i, upper_j = np.triu_indices(modes)
    quad = coords[upper_i, :] * coords[upper_j, :]
    return jnp.concatenate([coords, quad], axis=0).astype(jnp.bfloat16)


def on_device(snapshots, basis):
    partial_proj = lax.dot_general(
        basis, snapshots, (((0,), (0,)), ((), ())), preferred_element_type=jnp.float32
    )
    coords = lax.psum(partial_proj, "dof")
    features = build_features(coords)
    feature_count = features.shape[0]
    inverse_total = 1.0 / (features.shape[1] * lax.axis_size("tm"))
    owned_rows = feature_count // lax.axis_size("tm")
    col_width = feature_count // lax.axis_size("dof")
    col_start = lax.axis_index("dof") * col_width
    row_start = lax.axis_index("tm") * owned_rows
    initial = jnp.zeros((owned_rows, col_width), jnp.float32)
    piece = lax.all_gather(features, "tm", axis=1, tiled=True)
    row_part = lax.dynamic_slice_in_dim(piece, row_start, owned_rows, 0)
    col_part = lax.dynamic_slice_in_dim(piece, col_start, col_width, 0)
    product = lax.dot_general(
        row_part, col_part, (((1,), (1,)), ((), ())), preferred_element_type=jnp.float32
    )
    gram = initial + product * inverse_total
    return (gram, coords)


def solution(mesh):
    placed = (P("dof", "tm"), P("dof", None))
    return jax.shard_map(
        on_device,
        mesh=mesh,
        in_specs=placed,
        out_specs=(P("tm", "dof"), P(None, "tm")),
        check_vma=False,
    )
```

profile of v0, /device:TPU:0, one launch (start us, length us, event | category | flops | bytes accessed | tf_op | source)
XLA Modules:
  0.0 182.3 jit_solution(5816619657642350401)
XLA Ops:
  7.2 0.0 copy-start
  7.2 0.0 copy-start.2
  7.2 0.0 copy-start.3
  7.2 0.0 all-reduce.2.cloned.1.call-start
  7.2 1.7 copy-done
  8.9 6.4 %fusion.3 = f32[64,256]{1,0:T(8,128)} fusion(bf16[20480,64]{0,1:T(8,128)(2,1)S(1)} %copy-done, bf16[20480,256]{1,0:T(8,128)(2,1)} %param.6), kind=kOutput, calls=%fused_computation.10 | convolution fusion | flops 671088640 | bytes 13172736 | tf_op jit(solution)/shard_map/dot_general | solution.py:16
  15.3 0.0 all-reduce.2.cloned.1.call-update
  15.4 0.0 all-gather.2.cloned.1.call-start
  15.4 0.0 copy-done.2
  15.4 0.0 copy-done.3
  15.4 56.0 %all-reduce.2.cloned.1.call-done = f32[64,256]{1,0:T(8,128)} async-done(((f32[64,256]{1,0:T(8,128)}), f32[64,256]{1,0:T(8,128)}) %all-reduce.2.cloned.1.call-update) | async-done | bytes 65552 | tf_op jit(solution)/shard_map/psum | solution.py:19
  71.4 0.0 copy-start.1
  71.4 7.3 %gather_fusion = f32[2080,256]{1,0:T(8,128)} fusion(f32[64,256]{1,0:T(8,128)} %all-reduce.2.cloned.1.call-done, s32[3072]{0:T(1024)S(1)} %pad_clamp_fusion.1), kind=kCustom, calls=%fused_computation | custom fusion | bytes 4268160 | tf_op jit(solution)/shard_map/gather | solution.py:11
  78.7 0.0 copy-done.1
  78.7 6.4 %gather_fusion.1 = f32[2080,256]{1,0:T(8,128)} fusion(f32[64,256]{1,0:T(8,128)S(1)} %copy-done.1, s32[3072]{0:T(1024)S(1)} %pad_clamp_fusion), kind=kCustom, calls=%fused_computation.1 | custom fusion | bytes 4268160 | tf_op jit(solution)/shard_map/gather | solution.py:11
  85.0 2.5 %multiply_convert_fusion = bf16[2080,256]{1,0:T(8,128)(2,1)S(1)} fusion(f32[2080,256]{1,0:T(8,128)} %gather_fusion, f32[2080,256]{1,0:T(8,128)} %gather_fusion.1), kind=kLoop, calls=%fused_computation.2 | loop fusion | flops 1064960 | bytes 5324800 | tf_op jit(solution)/shard_map/convert.1
  87.5 1.1 pad_maximum_fusion
  88.6 0.0 all-gather.2.cloned.1.call-update
  88.6 83.3 %all-gather.2.cloned.1.call-done = bf16[2144,1024]{1,0:T(8,128)(2,1)} async-done(((bf16[2144,256]{1,0:T(8,128)(2,1)}), bf16[2144,1024]{1,0:T(8,128)(2,1)}) %all-gather.2.cloned.1.call-update) | async-done | bytes 4390928 | tf_op jit(solution)/shard_map/all_gather | solution.py:28
  171.9 2.9 %convolution_multiply_fusion = f32[536,268]{0,1:T(8,128)} fusion(bf16[2144,1024]{1,0:T(8,128)(2,1)} %all-gather.2.cloned.1.call-done, s32[]{:T(128)S(6)} %select_n.14, s32[]{:T(128)S(6)} %select_n.15), kind=kOutput, calls=%fused_computation.3 | convolution fusion | flops 294334752 | bytes 2229384 | tf_op jit(solution)/shard_map/dot_general | solution.py:31
  174.8 0.6 copy.9
  (3 shorter events, 0.0 us)
Async XLA Ops:
  7.2 1.7 copy-start
  7.2 8.2 %copy-start.2 = (s32[2080]{0:T(1024)S(1)}, s32[2080]{0:T(1024)}, u32[]{:S(2)}) copy-start(s32[2080]{0:T(1024)} %constant.32) | copy-start | bytes 24964
  7.2 8.2 %copy-start.3 = (s32[2080]{0:T(1024)S(1)}, s32[2080]{0:T(1024)}, u32[]{:S(2)}) copy-start(s32[2080]{0:T(1024)} %constant.33) | copy-start | bytes 24964
  7.2 64.2 %all-reduce.2.cloned.1.call-start = ((), (), s32[]{:S(2)}) async-start(), calls=%async_computation | async-start | bytes 131072 | tf_op jit(solution)/shard_map/psum | solution.py:19
  15.4 156.6 %all-gather.2.cloned.1.call-start = ((), (), s32[]{:S(2)}) async-start(), calls=%async_computation.1 | async-start | bytes 5488640 | tf_op jit(solution)/shard_map/all_gather | solution.py:28
  71.4 7.3 %copy-start.1 = (f32[64,256]{1,0:T(8,128)S(1)}, f32[64,256]{1,0:T(8,128)}, u32[]{:S(2)}) copy-start(f32[64,256]{1,0:T(8,128)} %all-reduce.2.cloned.1.call-done) | copy-start | bytes 196612
Sparse Core Ops, SparseCore 0:
  15.5 55.8 all-reduce.1
  88.7 83.1 all-gather.1
where the time goes:
time: 183 us; the launch traced here: 182 us
  waiting for transfers between devices  139 us (76%)
  local copies, waits for them, and re-layouts  15.9 us (9%)
  between operations  14.1 us (8%)
  matrix products  9.32 us (5%)
  other arithmetic  3.55 us (2%)
    all_gather x1, waiting for transfers between devices, on_device(): piece = lax.all_gather(features, 'tm', axis=1, tiled=True)  83.3 us
    psum x1, waiting for transfers between devices, on_device(): coords = lax.psum(partial_proj, 'dof')  56 us
    gather x2, local copies, waits for them, and re-layouts, build_features(): quad = coords[upper_i, :] * coords[upper_j, :]  13.6 us
    dot_general x1, matrix products, on_device(): lax.dot_general(basis, snapshots, (((0,), (0,)), ((), ())), preferred_ele...  6.42 us
  transfers between devices with their start and end apart: 2, of which 2 were waited for; matrix products, arithmetic and copies ran while one was open for 0% of the time, Pallas kernels for 0%

commit v1 on v0

--- a/solution.py
+++ b/solution.py
@@ -25,7 +25,7 @@
     col_start = lax.axis_index("dof") * col_width
     row_start = lax.axis_index("tm") * owned_rows
     initial = jnp.zeros((owned_rows, col_width), jnp.float32)
-    piece = lax.all_gather(features, "tm", axis=1, tiled=True)
+    piece = jnp.concatenate(lax.all_gather(features, "tm"), axis=1)
     row_part = lax.dynamic_slice_in_dim(piece, row_start, owned_rows, 0)
     col_part = lax.dynamic_slice_in_dim(piece, col_start, col_width, 0)
     product = lax.dot_general(

time: 183 us -> 190 us (1.038)
  local copies, waits for them, and re-layouts: 15.9 us -> 22.4 us
    reshape x0 -> x1, local copies, waits for them, and re-layouts: none -> 6.44 us  [on_device(): piece = jnp.concatenate(lax.all_gather(features, 'tm'), axis=1)]
    another operation x2 -> x0, other arithmetic: 2.46 us -> none
    concatenate x1 -> x3, other arithmetic: 1.08 us -> 3.53 us  [build_features(): return jnp.concatenate([coords, quad], axis=0).astype(jnp.bfloat16)]
where the time goes in v1:
time: 190 us
  waiting for transfers between devices  140 us (74%)
  local copies, waits for them, and re-layouts  22.4 us (12%)
  between operations  14.1 us (7%)
  matrix products  10.4 us (5%)
  other arithmetic  3.54 us (2%)
    all_gather x1, waiting for transfers between devices, on_device(): piece = jnp.concatenate(lax.all_gather(features, 'tm'), axis=1)  83.5 us
    psum x1, waiting for transfers between devices, on_device(): coords = lax.psum(partial_proj, 'dof')  55.9 us
    gather x2, local copies, waits for them, and re-layouts, build_features(): quad = coords[upper_i, :] * coords[upper_j, :]  13.6 us
    reshape x1, local copies, waits for them, and re-layouts, on_device(): piece = jnp.concatenate(lax.all_gather(features, 'tm'), axis=1)  6.44 us
    dot_general x1, matrix products, on_device(): lax.dot_general(basis, snapshots, (((0,), (0,)), ((), ())), preferred_ele...  6.44 us
    dot_general x1, matrix products, on_device(): lax.dot_general(row_part, col_part, (((1,), (1,)), ((), ())), preferred_e...  3.95 us
  transfers between devices with their start and end apart: 2, of which 2 were waited for; matrix products, arithmetic and copies ran while one was open for 0% of the time, Pallas kernels for 0%

profile of v1, /device:TPU:0, one launch (start us, length us, event | category | flops | bytes accessed | tf_op | source)
XLA Modules:
  0.0 190.0 jit_solution(8497530983714208273)
XLA Ops:
  7.2 0.0 copy-start
  7.2 0.0 copy-start.2
  7.2 0.0 copy-start.3
  7.2 0.0 all-reduce.2.cloned.1.call-start
  7.2 1.7 copy-done
  8.9 6.4 %fusion.8 = f32[64,256]{1,0:T(8,128)} fusion(bf16[20480,64]{0,1:T(8,128)(2,1)S(1)} %copy-done, bf16[20480,256]{1,0:T(8,128)(2,1)} %param.6), kind=kOutput, calls=%fused_computation.13 | convolution fusion | flops 671088640 | bytes 13172736 | tf_op jit(solution)/shard_map/dot_general | solution.py:16
  15.3 0.0 all-reduce.2.cloned.1.call-update
  15.4 0.0 all-gather.2.cloned.1.call-start
  15.4 0.0 copy-done.2
  15.4 0.0 copy-done.3
  15.5 55.9 %all-reduce.2.cloned.1.call-done = f32[64,256]{1,0:T(8,128)} async-done(((f32[64,256]{1,0:T(8,128)}), f32[64,256]{1,0:T(8,128)}) %all-reduce.2.cloned.1.call-update) | async-done | bytes 65552 | tf_op jit(solution)/shard_map/psum | solution.py:19
  71.4 0.0 copy-start.1
  71.4 7.3 %gather_fusion = f32[2080,256]{1,0:T(8,128)} fusion(f32[64,256]{1,0:T(8,128)} %all-reduce.2.cloned.1.call-done, s32[3072]{0:T(1024)S(1)} %pad_clamp_fusion.1), kind=kCustom, calls=%fused_computation | custom fusion | bytes 4268160 | tf_op jit(solution)/shard_map/gather | solution.py:11
  78.7 0.0 copy-done.1
  78.7 6.4 %gather_fusion.1 = f32[2080,256]{1,0:T(8,128)} fusion(f32[64,256]{1,0:T(8,128)S(1)} %copy-done.1, s32[3072]{0:T(1024)S(1)} %pad_clamp_fusion), kind=kCustom, calls=%fused_computation.1 | custom fusion | bytes 4268160 | tf_op jit(solution)/shard_map/gather | solution.py:11
  85.0 2.5 %fusion.5 = bf16[1,2080,256]{2,1,0:T(8,128)(2,1)S(1)} fusion(f32[2080,256]{1,0:T(8,128)} %gather_fusion, f32[2080,256]{1,0:T(8,128)} %gather_fusion.1), kind=kLoop, calls=%fused_computation.7 | loop fusion | flops 1064960 | bytes 5324800 | tf_op jit(solution)/shard_map/concatenate | solution.py:12
  87.5 1.1 pad_maximum_fusion
  88.6 0.0 all-gather.2.cloned.1.call-update
  88.6 83.5 %all-gather.2.cloned.1.call-done = bf16[4,2144,256]{2,1,0:T(8,128)(2,1)} async-done(((bf16[1,2144,256]{2,1,0:T(8,128)(2,1)}), bf16[4,2144,256]{2,1,0:T(8,128)(2,1)}) %all-gather.2.cloned.1.call-update) | async-done | bytes 4390928 | tf_op jit(solution)/shard_map/all_gather | solution.py:28
  172.1 6.4 %copy.9 = bf16[2144,4,256]{0,2,1:T(8,128)(2,1)} copy(bf16[2144,4,256]{2,0,1:T(8,128)(2,1)} %bitcast.9) | data formatting | bytes 8781824 | tf_op jit(solution)/shard_map/reshape | solution.py:28
  178.6 3.9 %fusion.2 = f32[536,268]{0,1:T(8,128)} fusion(bf16[2144,1024]{0,1:T(8,128)(2,1)} %bitcast.8, s32[]{:T(128)S(6)} %select_n.14, s32[]{:T(128)S(6)} %select_n.15), kind=kOutput, calls=%fused_computation.5 | convolution fusion | flops 294334752 | bytes 2671752 | tf_op jit(solution)/shard_map/dot_general | solution.py:31
  182.5 0.6 copy.11
  (3 shorter events, 0.0 us)
Async XLA Ops:
  7.2 1.7 copy-start
  7.2 8.2 %copy-start.2 = (s32[2080]{0:T(1024)S(1)}, s32[2080]{0:T(1024)}, u32[]{:S(2)}) copy-start(s32[2080]{0:T(1024)} %constant.32) | copy-start | bytes 24964
  7.2 8.3 %copy-start.3 = (s32[2080]{0:T(1024)S(1)}, s32[2080]{0:T(1024)}, u32[]{:S(2)}) copy-start(s32[2080]{0:T(1024)} %constant.33) | copy-start | bytes 24964
  7.2 64.2 %all-reduce.2.cloned.1.call-start = ((), (), s32[]{:S(2)}) async-start(), calls=%async_computation | async-start | bytes 131072 | tf_op jit(solution)/shard_map/psum | solution.py:19
  15.4 156.8 %all-gather.2.cloned.1.call-start = ((), (), s32[]{:S(2)}) async-start(), calls=%async_computation.1 | async-start | bytes 5488640 | tf_op jit(solution)/shard_map/all_gather | solution.py:28
  71.4 7.3 %copy-start.1 = (f32[64,256]{1,0:T(8,128)S(1)}, f32[64,256]{1,0:T(8,128)}, u32[]{:S(2)}) copy-start(f32[64,256]{1,0:T(8,128)} %all-reduce.2.cloned.1.call-done) | copy-start | bytes 196612
Sparse Core Ops, SparseCore 0:
  15.5 55.8 all-reduce.1
  88.7 83.3 all-gather.1

commit v2 on v0

--- a/solution.py
+++ b/solution.py
@@ -16,7 +16,7 @@
     partial_proj = lax.dot_general(
         basis, snapshots, (((0,), (0,)), ((), ())), preferred_element_type=jnp.float32
     )
-    coords = lax.psum(partial_proj, "dof")
+    coords = jnp.sum(lax.all_gather(partial_proj, "dof"), axis=0)
     features = build_features(coords)
     feature_count = features.shape[0]
     inverse_total = 1.0 / (features.shape[1] * lax.axis_size("tm"))

time: 183 us -> 137 us (0.75)
  waiting for transfers between devices: 139 us -> 84.2 us
  blocking collectives: 0 us -> 11.3 us
    psum x1 -> x0, waiting for transfers between devices: 56 us -> none  [on_device(): coords = lax.psum(partial_proj, 'dof')]
    all_gather x0 -> x1, blocking collectives: none -> 11.3 us  [on_device(): coords = jnp.sum(lax.all_gather(partial_proj, 'dof'), axis=0)]
  transfers between devices with their start and end apart: 2 -> 1, of which waited for: 2 -> 1; matrix products, arithmetic and copies ran while one was open for 0% -> 0% of each run, Pallas kernels for 0% -> 0%
where the time goes in v2:
time: 137 us; the launch traced here: 136 us
  waiting for transfers between devices  84.2 us (61%)
  local copies, waits for them, and re-layouts  14.4 us (11%)
  between operations  14.1 us (10%)
  blocking collectives  11.3 us (8%)
  matrix products  8.67 us (6%)
  other arithmetic  3.57 us (3%)
    all_gather x1, waiting for transfers between devices, on_device(): piece = lax.all_gather(features, 'tm', axis=1, tiled=True)  84.2 us
    gather x2, local copies, waits for them, and re-layouts, build_features(): quad = coords[upper_i, :] * coords[upper_j, :]  12.7 us
    all_gather x1, blocking collectives, on_device(): coords = jnp.sum(lax.all_gather(partial_proj, 'dof'), axis=0)  11.3 us
    dot_general x1, matrix products, on_device(): lax.dot_general(basis, snapshots, (((0,), (0,)), ((), ())), preferred_ele...  5.78 us
    dot_general x1, matrix products, on_device(): lax.dot_general(row_part, col_part, (((1,), (1,)), ((), ())), preferred_e...  2.89 us
  transfers between devices with their start and end apart: 1, of which 1 were waited for; matrix products, arithmetic and copies ran while one was open for 0% of the time, Pallas kernels for 0%

profile of v2, /device:TPU:0, one launch (start us, length us, event | category | flops | bytes accessed | tf_op | source)
XLA Modules:
  0.0 136.4 jit_solution(1558212727610732517)
XLA Ops:
  7.2 0.0 copy-start
  7.2 0.0 copy-start.3
  7.2 0.0 all-gather.3.cloned.1.call-start
  7.2 1.7 %copy-done = bf16[20480,64]{0,1:T(8,128)(2,1)S(1)} copy-done((bf16[20480,64]{0,1:T(8,128)(2,1)S(1)}, bf16[20480,64]{0,1:T(8,128)(2,1)}, u32[]{:S(2)}) %copy-start) | copy-done | bytes 2621464
  8.9 5.8 %fusion.3 = f32[64,256]{1,0:T(8,128)S(1)} fusion(bf16[20480,64]{0,1:T(8,128)(2,1)S(1)} %copy-done, bf16[20480,256]{1,0:T(8,128)(2,1)} %param.6), kind=kOutput, calls=%fused_computation.10 | convolution fusion | flops 671088640 | bytes 13172736 | tf_op jit(solution)/shard_map/dot_general | solution.py:16
  14.7 11.3 %all-gather = f32[512,256]{1,0:T(8,128)S(1)} all-gather(f32[64,256]{1,0:T(8,128)S(1)} %fusion.3), channel_id=2, replica_groups=mesh['dof'=8,'tm'=4] {'dof'}, dimensions={0}, use_global_device_ids=true | all-gather | bytes 589824 | tf_op jit(solution)/shard_map/all_gather | solution.py:19
  26.0 0.0 copy-done.3
  26.1 0.0 copy-start.1
  26.1 0.0 copy-start.2
  26.1 6.4 %gather_fusion = f32[2080,256]{1,0:T(8,128)} fusion(f32[64,256]{1,0:T(8,128)S(1)} %reduce_sum.9, s32[3072]{0:T(1024)S(1)} %pad_clamp_fusion.1), kind=kCustom, calls=%fused_computation | custom fusion | bytes 4268160 | tf_op jit(solution)/shard_map/gather | solution.py:11
  32.5 0.0 copy-done.2
  32.5 0.0 copy-done.1
  32.5 6.4 %gather_fusion.1 = f32[2080,256]{1,0:T(8,128)} fusion(f32[64,256]{1,0:T(8,128)S(1)} %reduce_sum.9, s32[3072]{0:T(1024)S(1)} %pad_clamp_fusion), kind=kCustom, calls=%fused_computation.1 | custom fusion | bytes 4268160 | tf_op jit(solution)/shard_map/gather | solution.py:11
  38.9 2.5 %multiply_convert_fusion = bf16[2080,256]{1,0:T(8,128)(2,1)S(1)} fusion(f32[2080,256]{1,0:T(8,128)} %gather_fusion, f32[2080,256]{1,0:T(8,128)} %gather_fusion.1), kind=kLoop, calls=%fused_computation.2 | loop fusion | flops 1064960 | bytes 5324800 | tf_op jit(solution)/shard_map/convert.1
  41.4 1.1 pad_maximum_fusion
  42.4 0.0 all-gather.3.cloned.1.call-update
  42.4 84.2 %all-gather.3.cloned.1.call-done = bf16[2144,1024]{1,0:T(8,128)(2,1)} async-done(((bf16[2144,256]{1,0:T(8,128)(2,1)}), bf16[2144,1024]{1,0:T(8,128)(2,1)}) %all-gather.3.cloned.1.call-update) | async-done | bytes 4390928 | tf_op jit(solution)/shard_map/all_gather | solution.py:28
  126.6 2.9 %convolution_multiply_fusion = f32[536,268]{0,1:T(8,128)} fusion(bf16[2144,1024]{1,0:T(8,128)(2,1)} %all-gather.3.cloned.1.call-done, s32[]{:T(128)S(6)} %select_n.14, s32[]{:T(128)S(6)} %select_n.15), kind=kOutput, calls=%fused_computation.3 | convolution fusion | flops 294334752 | bytes 2229384 | tf_op jit(solution)/shard_map/dot_general | solution.py:31
  (4 shorter events, 0.1 us)
Async XLA Ops:
  7.2 1.7 %copy-start = (bf16[20480,64]{0,1:T(8,128)(2,1)S(1)}, bf16[20480,64]{0,1:T(8,128)(2,1)}, u32[]{:S(2)}) copy-start(bf16[20480,64]{0,1:T(8,128)(2,1)} %param.7) | copy-start | bytes 7864324
  7.2 18.9 %copy-start.3 = (s32[2080]{0:T(1024)S(1)}, s32[2080]{0:T(1024)}, u32[]{:S(2)}) copy-start(s32[2080]{0:T(1024)} %constant.34) | copy-start | bytes 24964
  7.2 119.5 %all-gather.3.cloned.1.call-start = ((), (), s32[]{:S(2)}) async-start(), calls=%async_computation | async-start | bytes 5488640 | tf_op jit(solution)/shard_map/all_gather | solution.py:28
  26.1 6.4 %copy-start.1 = (f32[64,256]{1,0:T(8,128)}, f32[64,256]{1,0:T(8,128)S(1)}, u32[]{:S(2)}) copy-start(f32[64,256]{1,0:T(8,128)S(1)} %reduce_sum.9) | copy-start | bytes 196612
  26.1 6.4 %copy-start.2 = (s32[2080]{0:T(1024)S(1)}, s32[2080]{0:T(1024)}, u32[]{:S(2)}) copy-start(s32[2080]{0:T(1024)} %constant.35) | copy-start | bytes 24964
Sparse Core Ops, SparseCore 0:
  42.6 84.0 all-gather.2
